TPU v7x, 32 devices: a whole 2x2x4 slice. The times are simulated.
32 devices in a mesh: groups: 2 (over y), expert: 4 (over z), mp: 4 (over x, core).
Axes of the slice: x: 2, y: 2, z: 4, core: 2. Of those that a mesh axis runs over, the one named last changes fastest.
Arguments:
- tokens: bfloat16 [6144, 1024], P(('groups', 'expert'), 'mp'), parts along dimension 0, may hold values from -60 to 60
- gain: float32 [1024], replicated, may hold values from 0.1 to 1.9
- w_res_in: bfloat16 [1024, 4096], P(None, 'mp'), may hold values from -0.1875 to 0.1875
- w_res_out: bfloat16 [4096, 1024], P('mp'), may hold values from -0.09375 to 0.09375
- w_exp_in: bfloat16 [4, 1024, 4096], P('expert', None, 'mp'), may hold values from -0.1875 to 0.1875
- w_exp_out: bfloat16 [4, 4096, 1024], P('expert', 'mp'), may hold values from -0.09375 to 0.09375
- expert_of: int32 [6144], P(('groups', 'expert')), parts along dimension 0, may hold values from 0 to 3
- slot_of: int32 [6144], P(('groups', 'expert')), parts along dimension 0, may hold values from -1 to 239, as said below
- gate_prob: float32 [6144], P(('groups', 'expert')), parts along dimension 0, may hold values from 0.2 to 1
Outputs:
- layer_out: bfloat16 [6144, 1024], P(('groups', 'expert'), 'mp'), parts along dimension 0
There are 2 independent parts, one for each index of `groups`. A program takes and returns all parts, laid end to end along the dimension named above; an argument that names none is the same for every part. Nothing has to cross between parts.
Inputs may be any that keep to these rules, and one draw needn't show every extreme that they name: slot_of[t] is the number of earlier tokens of t's aligned block of 768 tokens with the same expert_of, or -1 where that number is 240 or more. In every draw one expert has more than 240 tokens in every aligned block.
All inputs are finite; a program needn't handle non-finite values.
Results may differ from a plain program's by a relative error of at most 0.014.
Values may be sent and summed in bfloat16 or wider, within the bound.
A program may use at most 64 MiB of HBM per device.

v0:
```python
import jax
import jax.numpy as jnp
from jax import lax
from jax.sharding import PartitionSpec as P


def rms_rows(tokens, gain):
    values = tokens.astype(jnp.float32)
    inverse = lax.rsqrt(jnp.mean(values * values, axis=-1, keepdims=True) + 1e-05)
    return (values * inverse * gain).astype(jnp.bfloat16)


def per_device(
    tokens, gain, w_res_in, w_res_out, w_exp_in, w_exp_out, expert_of, slot_of, gate_prob
):
    full_rows = lax.all_gather(tokens, "mp", axis=1, tiled=True)
    normed = rms_rows(full_rows, gain)
    res_hidden = jax.nn.gelu(jnp.dot(normed, w_res_in, preferred_element_type=jnp.float32)).astype(
        jnp.bfloat16
    )
    res_part = jnp.dot(res_hidden, w_res_out, preferred_element_type=jnp.float32)
    row_count = expert_of.shape[0]
    experts = lax.axis_size("expert")
    capacity = max(2, 5 * row_count // (4 * experts))
    feat_width = tokens.shape[1]
    slot_id = jnp.where(slot_of >= 0, expert_of * capacity + slot_of, -1)
    slot_index = jnp.arange(experts * capacity, dtype=jnp.int32)
    send_table = (slot_index[:, None] == slot_id[None, :]).astype(jnp.bfloat16)
    take_table = (slot_id[:, None] == slot_index[None, :]).astype(jnp.bfloat16)
    local_in = w_exp_in[0]
    local_out = w_exp_out[0]
    mp_index = lax.axis_index("mp")
    own_slice = lax.dynamic_slice_in_dim(normed, mp_index * feat_width, feat_width, 1)
    outgoing = jnp.dot(send_table, own_slice, preferred_element_type=jnp.float32).astype(
        jnp.bfloat16
    )
    incoming = lax.all_to_all(
        outgoing.reshape(experts, capacity, feat_width),
        "expert",
        split_axis=0,
        concat_axis=0,
        tiled=True,
    )
    piece = lax.all_gather(incoming, "mp", axis=2, tiled=True)
    flat_piece = piece.reshape(-1, piece.shape[2])
    preact = jnp.dot(flat_piece, local_in, preferred_element_type=jnp.float32)
    exp_hidden = jax.nn.gelu(preact).astype(jnp.bfloat16)
    exp_part = jnp.dot(exp_hidden, local_out, preferred_element_type=jnp.float32)
    gate_column = gate_prob[:, None]
    summed = lax.psum_scatter(exp_part.astype(jnp.bfloat16), "mp", scatter_dimension=1, tiled=True)
    returned = lax.all_to_all(
        summed.reshape(experts, capacity, feat_width),
        "expert",
        split_axis=0,
        concat_axis=0,
        tiled=True,
    )
    moe_value = jnp.dot(
        take_table,
        returned.reshape(experts * capacity, feat_width),
        preferred_element_type=jnp.float32,
    )
    res_sum = lax.psum_scatter(
        res_part.astype(jnp.bfloat16), "mp", scatter_dimension=1, tiled=True
    ).astype(jnp.float32)
    return (res_sum + gate_column * moe_value).astype(jnp.bfloat16)


def solution(mesh):
    return jax.shard_map(
        per_device,
        mesh=mesh,
        in_specs=(
            P(("groups", "expert"), "mp"),
            P(),
            P(None, "mp"),
            P("mp", None),
            P("expert", None, "mp"),
            P("expert", "mp", None),
            P(("groups", "expert")),
            P(("groups", "expert")),
            P(("groups", "expert")),
        ),
        out_specs=P(("groups", "expert"), "mp"),
        check_vma=False,
    )
```

profile of v0, /device:TPU:0, one launch (start us, length us, event | category | flops | bytes accessed | tf_op | source)
XLA Modules:
  0.0 153.2 jit_solution(7485082166365213157)
XLA Ops:
  6.5 0.0 copy-start
  6.5 0.0 all-gather.3.cloned.1.call-start
  6.5 0.7 all-gather.3.cloned.1.call-update
  7.3 0.0 all-gather.5.cloned.1.call-start
  7.3 0.7 add_select_fusion
  8.0 23.4 %all-gather.3.cloned.1.call-done = bf16[768,1024]{1,0:T(8,128)(2,1)} async-done(((bf16[768,256]{1,0:T(8,128)(2,1)}), bf16[768,1024]{1,0:T(8,128)(2,1)}) %all-gather.3.cloned.1.call-update) | async-done | bytes 1572880 | tf_op jit(solution)/shard_map/all_gather | solution.py:16
  31.5 0.0 copy-start.1
  31.5 1.9 %fusion.8 = f32[768]{0:T(1024)S(1)} fusion(bf16[768,1024]{1,0:T(8,128)(2,1)} %all-gather.3.cloned.1.call-done), kind=kLoop, calls=%fused_computation.12 | loop fusion | flops 2358528 | bytes 1575936 | tf_op jit(solution)/shard_map/reduce_sum | solution.py:9
  33.4 0.0 copy-done.1
  33.4 1.1 fusion.10
  34.5 0.0 copy-start.2
  34.5 1.1 copy-done.2
  35.6 0.6 fusion.39
  36.3 18.7 %all_to_all.10 = bf16[4,240,256]{2,1,0:T(8,128)(2,1)} all-to-all(bf16[4,240,256]{2,1,0:T(8,128)(2,1)S(1)} %bitcast.23), channel_id=1, replica_groups=mesh['groups'=2,'expert'=4,'mp'=4] {'expert'}, dimensions={0} | all-to-all | bytes 983040 | tf_op jit(solution)/shard_map/all_to_all | solution.py:37
  55.0 0.0 all-gather.5.cloned.1.call-update
  55.0 0.0 reduce-scatter.5.cloned.1.call-start
  55.1 20.3 %all-gather.5.cloned.1.call-done = bf16[4,240,1024]{2,1,0:T(8,128)(2,1)} async-done(((bf16[4,240,256]{2,1,0:T(8,128)(2,1)}), bf16[4,240,1024]{2,1,0:T(8,128)(2,1)}) %all-gather.5.cloned.1.call-update) | async-done | bytes 1966096 | tf_op jit(solution)/shard_map/all_gather | solution.py:44
  75.4 0.0 copy-done
  75.4 7.8 %fusion.27 = bf16[960,1024]{1,0:T(8,128)(2,1)} fusion(bf16[1,1024,1024]{2,1,0:T(8,128)(2,1)S(1)} %copy-done, bf16[960,1024]{1,0:T(8,128)(2,1)} %bitcast.24, bf16[1,1024,1024]{2,1,0:T(8,128)(2,1)} %param.13), kind=kOutput, calls=%fused_computation.31 | convolution fusion | flops 4036362240 | bytes 8126464 | tf_op jit(solution)/shard_map/dot_general | solution.py:48
  83.2 0.0 reduce-scatter.5.cloned.1.call-update
  83.2 0.0 reduce-scatter.3.cloned.1.call-start
  83.2 7.4 %convolution_convert_fusion = bf16[768,1024]{1,0:T(8,128)(2,1)} fusion(bf16[1024,1024]{1,0:T(8,128)(2,1)} %param.12, bf16[768,1024]{1,0:T(8,128)(2,1)} %copy-done.2, bf16[1024,1024]{1,0:T(8,128)(2,1)} %param.11), kind=kOutput, calls=%fused_computation.32 | convolution fusion | flops 3229089792 | bytes 7340032 | tf_op jit(solution)/shard_map/dot_general | solution.py:21
  90.6 0.0 copy-start.3
  90.6 0.0 reduce-scatter.3.cloned.1.call-update
  90.6 23.1 %reduce-scatter.5.cloned.1.call-done = bf16[960,256]{1,0:T(8,128)(2,1)} async-done(((bf16[960,1024]{1,0:T(8,128)(2,1)}), bf16[960,256]{1,0:T(8,128)(2,1)}) %reduce-scatter.5.cloned.1.call-update) | async-done | bytes 491536 | tf_op jit(solution)/shard_map/reduce_scatter | solution.py:50
  113.7 4.6 %all-to-all-start.1 = ((bf16[4,240,256]{2,1,0:T(8,128)(2,1)}), bf16[4,240,256]{2,1,0:T(8,128)(2,1)S(1)}, u32[]{:S(2)}, u32[]{:S(2)}) async-start(bf16[4,240,256]{2,1,0:T(8,128)(2,1)} %bitcast.21), calls=%async_computation.3 | async-start | bytes 983040 | tf_op jit(solution)/shard_map/all_to_all | solution.py:51
  118.3 25.8 %reduce-scatter.3.cloned.1.call-done = bf16[768,256]{1,0:T(8,128)(2,1)} async-done(((bf16[768,1024]{1,0:T(8,128)(2,1)}), bf16[768,256]{1,0:T(8,128)(2,1)}) %reduce-scatter.3.cloned.1.call-update) | async-done | bytes 393232 | tf_op jit(solution)/shard_map/reduce_scatter | solution.py:63
  144.2 0.0 all-to-all-done.1
  144.2 0.0 copy-done.3
  144.2 2.5 %fusion.40 = bf16[768,256]{1,0:T(8,128)(2,1)} fusion(bf16[960,256]{1,0:T(8,128)(2,1)S(1)} %bitcast.22, s32[768]{0:T(1024)S(1)} %add_select_fusion, bf16[768,256]{1,0:T(8,128)(2,1)} %reduce-scatter.3.cloned.1.call-done, f32[768]{0:T(1024)S(1)} %copy-done.3), kind=kOutput, calls=%fused_computation.42 | convolution fusion | flops 379011072 | bytes 1284096 | tf_op jit(solution)/shard_map/dot_general | solution.py:58
  (1 shorter events, 0.0 us)
Async XLA Ops:
  6.5 68.9 %copy-start = (bf16[1,1024,1024]{2,1,0:T(8,128)(2,1)S(1)}, bf16[1,1024,1024]{2,1,0:T(8,128)(2,1)}, u32[]{:S(2)}) copy-start(bf16[1,1024,1024]{2,1,0:T(8,128)(2,1)} %param.14) | copy-start | bytes 6291460
  6.5 24.9 %all-gather.3.cloned.1.call-start = ((), (), s32[]{:S(2)}) async-start(), calls=%async_computation.4 | async-start | bytes 1966080 | tf_op jit(solution)/shard_map/all_gather | solution.py:16
  7.3 68.1 %all-gather.5.cloned.1.call-start = ((), (), s32[]{:S(2)}) async-start(), calls=%async_computation.6 | async-start | bytes 2457600 | tf_op jit(solution)/shard_map/all_gather | solution.py:44
  31.5 1.9 %copy-start.1 = (bf16[768,1024]{1,0:T(8,128)(2,1)S(1)}, bf16[768,1024]{1,0:T(8,128)(2,1)}, u32[]{:S(2)}) copy-start(bf16[768,1024]{1,0:T(8,128)(2,1)} %all-gather.3.cloned.1.call-done) | copy-start | bytes 4718596
  34.5 1.1 copy-start.2
  55.0 58.7 %reduce-scatter.5.cloned.1.call-start = ((), (), s32[]{:S(2)}) async-start(), calls=%async_computation.7 | async-start | bytes 2457600 | tf_op jit(solution)/shard_map/reduce_scatter | solution.py:50
  83.2 61.0 %reduce-scatter.3.cloned.1.call-start = ((), (), s32[]{:S(2)}) async-start(), calls=%async_computation.5 | async-start | bytes 1966080 | tf_op jit(solution)/shard_map/reduce_scatter | solution.py:63
  90.6 53.6 %copy-start.3 = (f32[768]{0:T(1024)S(1)}, f32[768]{0:T(1024)}, u32[]{:S(2)}) copy-start(f32[768]{0:T(1024)} %param.17) | copy-start | bytes 9220
  113.7 30.5 %all-to-all-start.1 = ((bf16[4,240,256]{2,1,0:T(8,128)(2,1)}), bf16[4,240,256]{2,1,0:T(8,128)(2,1)S(1)}, u32[]{:S(2)}, u32[]{:S(2)}) async-start(bf16[4,240,256]{2,1,0:T(8,128)(2,1)} %bitcast.21), calls=%async_computation.3 | async-start | bytes 983040 | tf_op jit(solution)/shard_map/all_to_all | solution.py:51
Sparse Core Ops, SparseCore 0:
  8.9 22.5 all-gather.2
  55.2 20.1 all-gather.4
  83.3 30.3 reduce-scatter.4
  116.1 28.0 reduce-scatter.2
where the time goes:
time: 154 us; the launch traced here: 153 us
  waiting for transfers between devices  93.4 us (61%)
  blocking collectives  18.7 us (12%)
  matrix products  18.3 us (12%)
  between operations  13.2 us (9%)
  starting transfers between devices  4.75 us (3%)
  other arithmetic  3.73 us (2%)
    reduce_scatter x1, waiting for transfers between devices, per_device(): lax.psum_scatter(res_part.astype(jnp.bfloat16), 'mp', scatter_dimension=1...  25.8 us
    all_gather x1, waiting for transfers between devices, per_device(): full_rows = lax.all_gather(tokens, 'mp', axis=1, tiled=True)  23.4 us
    reduce_scatter x1, waiting for transfers between devices, per_device(): lax.psum_scatter(exp_part.astype(jnp.bfloat16), 'mp', scatter_dimension=1...  23.1 us
    all_gather x1, waiting for transfers between devices, per_device(): piece = lax.all_gather(incoming, 'mp', axis=2, tiled=True)  20.3 us
    all_to_all x1, blocking collectives, per_device(): lax.all_to_all(outgoing.reshape(experts, capacity, feat_width), 'expert',...  18.7 us
    dot_general x1, matrix products, per_device(): jnp.dot(exp_hidden, local_out, preferred_element_type=jnp.float32)  7.77 us
    dot_general x1, matrix products, per_device(): jnp.dot(res_hidden, w_res_out, preferred_element_type=jnp.float32)  7.35 us
    all_to_all x1, starting transfers between devices, per_device(): lax.all_to_all(summed.reshape(experts, capacity, feat_width), 'expert', s...  4.62 us
  transfers between devices with their start and end apart: 5, of which 4 were waited for; matrix products, arithmetic and copies ran while one was open for 5% of the time, Pallas kernels for 0%

commit v1 on v0

--- a/solution.py
+++ b/solution.py
@@ -13,7 +13,7 @@
 def per_device(
     tokens, gain, w_res_in, w_res_out, w_exp_in, w_exp_out, expert_of, slot_of, gate_prob
 ):
-    full_rows = lax.all_gather(tokens, "mp", axis=1, tiled=True)
+    full_rows = jnp.concatenate(lax.all_gather(tokens, "mp"), 1)
     normed = rms_rows(full_rows, gain)
     res_hidden = jax.nn.gelu(jnp.dot(normed, w_res_in, preferred_element_type=jnp.float32)).astype(
         jnp.bfloat16

time: 154 us -> 161 us (1.045)
  other arithmetic: 3.73 us -> 8.02 us
  local copies, waits for them, and re-layouts: 1.15 us -> 4.77 us
    convert_element_type x0 -> x1, local copies, waits for them, and re-layouts: none -> 3.58 us  [rms_rows(): values = tokens.astype(jnp.float32)]
    convert_element_type x0 -> x1, other arithmetic: none -> 3.32 us  [rms_rows(): values = tokens.astype(jnp.float32)]
where the time goes in v1:
time: 161 us
  waiting for transfers between devices  92.9 us (58%)
  matrix products  18.7 us (12%)
  blocking collectives  18.7 us (12%)
  between operations  13.2 us (8%)
  other arithmetic  8.02 us (5%)
  local copies, waits for them, and re-layouts  4.77 us (3%)
  starting transfers between devices  4.72 us (3%)
    reduce_scatter x1, waiting for transfers between devices, per_device(): lax.psum_scatter(res_part.astype(jnp.bfloat16), 'mp', scatter_dimension=1...  25.8 us
    all_gather x1, waiting for transfers between devices, per_device(): full_rows = jnp.concatenate(lax.all_gather(tokens, 'mp'), 1)  23.3 us
    reduce_scatter x1, waiting for transfers between devices, per_device(): lax.psum_scatter(exp_part.astype(jnp.bfloat16), 'mp', scatter_dimension=1...  22.7 us
    all_gather x1, waiting for transfers between devices, per_device(): piece = lax.all_gather(incoming, 'mp', axis=2, tiled=True)  20.3 us
    all_to_all x1, blocking collectives, per_device(): lax.all_to_all(outgoing.reshape(experts, capacity, feat_width), 'expert',...  18.7 us
    dot_general x1, matrix products, per_device(): jnp.dot(exp_hidden, local_out, preferred_element_type=jnp.float32)  7.81 us
    dot_general x1, matrix products, per_device(): jnp.dot(res_hidden, w_res_out, preferred_element_type=jnp.float32)  7.74 us
    all_to_all x1, starting transfers between devices, per_device(): lax.all_to_all(summed.reshape(experts, capacity, feat_width), 'expert', s...  4.6 us
  transfers between devices with their start and end apart: 5, of which 4 were waited for; matrix products, arithmetic and copies ran while one was open for 5% of the time, Pallas kernels for 0%

profile of v1, /device:TPU:0, one launch (start us, length us, event | category | flops | bytes accessed | tf_op | source)
XLA Modules:
  0.0 160.9 jit_solution(12388165496052242017)
XLA Ops:
  6.5 0.0 copy-start
  6.5 0.0 all-gather.6.cloned.1.call-start
  6.5 0.7 all-gather.6.cloned.1.call-update
  7.3 0.0 all-gather.4.cloned.1.call-start
  7.3 0.7 add_select_fusion
  8.0 23.3 %all-gather.6.cloned.1.call-done = bf16[3072,256]{1,0:T(8,128)(2,1)} async-done(((bf16[768,256]{1,0:T(8,128)(2,1)}), bf16[3072,256]{1,0:T(8,128)(2,1)}) %all-gather.6.cloned.1.call-update) | async-done | bytes 1572880 | tf_op jit(solution)/shard_map/all_gather | solution.py:16
  31.3 1.8 %fusion.8 = f32[768]{0:T(1024)S(1)} fusion(bf16[4,768,256]{2,1,0:T(8,128)(2,1)} %bitcast.31), kind=kLoop, calls=%fused_computation.12 | loop fusion | flops 2358528 | bytes 1575936 | tf_op jit(solution)/shard_map/reduce_sum | solution.py:9
  33.1 3.3 %convert_bitcast_fusion = f32[768,4,256]{2,0,1:T(8,128)} fusion(bf16[4,768,256]{2,1,0:T(8,128)(2,1)} %bitcast.32), kind=kLoop, calls=%fused_computation.11 | loop fusion | flops 786432 | bytes 4718592 | tf_op jit(solution)/shard_map/convert_element_type | solution.py:8
  36.4 0.0 copy-start.2
  36.4 3.6 %copy.10 = f32[768,4,256]{0,2,1:T(8,128)} copy(f32[768,4,256]{2,0,1:T(8,128)} %convert_bitcast_fusion) | data formatting | bytes 6291456 | tf_op jit(solution)/shard_map/convert_element_type | solution.py:8
  40.0 0.0 copy-done.2
  40.0 2.2 %fusion.18 = bf16[768,1024]{0,1:T(8,128)(2,1)S(1)} fusion(f32[768,4,256]{0,2,1:T(8,128)} %copy.10, f32[1024]{0:T(1024)S(1)} %copy-done.2, f32[768]{0:T(1024)S(1)} %add_rsqrt_fusion), kind=kLoop, calls=%fused_computation.23 | loop fusion | flops 2359296 | bytes 4725760 | tf_op jit(solution)/shard_map/convert_element_type | solution.py:10
  42.2 0.0 copy-start.1
  42.2 1.2 copy-done.1
  43.4 0.6 fusion.39
  44.0 18.7 %all_to_all.10 = bf16[4,240,256]{2,1,0:T(8,128)(2,1)} all-to-all(bf16[4,240,256]{2,1,0:T(8,128)(2,1)S(1)} %bitcast.35), channel_id=1, replica_groups=mesh['groups'=2,'expert'=4,'mp'=4] {'expert'}, dimensions={0} | all-to-all | bytes 983040 | tf_op jit(solution)/shard_map/all_to_all | solution.py:37
  62.7 0.0 all-gather.4.cloned.1.call-update
  62.7 0.0 reduce-scatter.5.cloned.1.call-start
  62.8 20.3 %all-gather.4.cloned.1.call-done = bf16[4,240,1024]{2,1,0:T(8,128)(2,1)} async-done(((bf16[4,240,256]{2,1,0:T(8,128)(2,1)}), bf16[4,240,1024]{2,1,0:T(8,128)(2,1)}) %all-gather.4.cloned.1.call-update) | async-done | bytes 1966096 | tf_op jit(solution)/shard_map/all_gather | solution.py:44
  83.1 0.0 copy-done
  83.1 7.8 %fusion.27 = bf16[960,1024]{1,0:T(8,128)(2,1)} fusion(bf16[1,1024,1024]{2,1,0:T(8,128)(2,1)S(1)} %copy-done, bf16[960,1024]{1,0:T(8,128)(2,1)} %bitcast.36, bf16[1,1024,1024]{2,1,0:T(8,128)(2,1)} %param.13), kind=kOutput, calls=%fused_computation.32 | convolution fusion | flops 4036362240 | bytes 8126464 | tf_op jit(solution)/shard_map/dot_general | solution.py:48
  90.9 0.0 reduce-scatter.5.cloned.1.call-update
  90.9 0.0 copy-start.3
  90.9 0.0 reduce-scatter.3.cloned.1.call-start
  91.0 7.7 %convolution_convert_fusion = bf16[768,1024]{1,0:T(8,128)(2,1)} fusion(bf16[1024,1024]{1,0:T(8,128)(2,1)} %param.12, bf16[768,1024]{0,1:T(8,128)(2,1)} %copy-done.1, bf16[1024,1024]{1,0:T(8,128)(2,1)} %param.11), kind=kOutput, calls=%fused_computation.33 | convolution fusion | flops 3229089792 | bytes 7340032 | tf_op jit(solution)/shard_map/dot_general | solution.py:21
  98.7 0.0 reduce-scatter.3.cloned.1.call-update
  98.7 22.7 %reduce-scatter.5.cloned.1.call-done = bf16[960,256]{1,0:T(8,128)(2,1)} async-done(((bf16[960,1024]{1,0:T(8,128)(2,1)}), bf16[960,256]{1,0:T(8,128)(2,1)}) %reduce-scatter.5.cloned.1.call-update) | async-done | bytes 491536 | tf_op jit(solution)/shard_map/reduce_scatter | solution.py:50
  121.5 4.6 %all-to-all-start.1 = ((bf16[4,240,256]{2,1,0:T(8,128)(2,1)}), bf16[4,240,256]{2,1,0:T(8,128)(2,1)S(1)}, u32[]{:S(2)}, u32[]{:S(2)}) async-start(bf16[4,240,256]{2,1,0:T(8,128)(2,1)} %bitcast.33), calls=%async_computation.3 | async-start | bytes 983040 | tf_op jit(solution)/shard_map/all_to_all | solution.py:51
  126.0 25.8 %reduce-scatter.3.cloned.1.call-done = bf16[768,256]{1,0:T(8,128)(2,1)} async-done(((bf16[768,1024]{1,0:T(8,128)(2,1)}), bf16[768,256]{1,0:T(8,128)(2,1)}) %reduce-scatter.3.cloned.1.call-update) | async-done | bytes 393232 | tf_op jit(solution)/shard_map/reduce_scatter | solution.py:63
  151.9 0.0 all-to-all-done.1
  151.9 0.0 copy-done.3
  151.9 2.5 %fusion.40 = bf16[768,256]{1,0:T(8,128)(2,1)} fusion(bf16[960,256]{1,0:T(8,128)(2,1)S(1)} %bitcast.34, s32[768]{0:T(1024)S(1)} %add_select_fusion, bf16[768,256]{1,0:T(8,128)(2,1)} %reduce-scatter.3.cloned.1.call-done, f32[768]{0:T(1024)S(1)} %copy-done.3), kind=kOutput, calls=%fused_computation.43 | convolution fusion | flops 379011072 | bytes 1284096 | tf_op jit(solution)/shard_map/dot_general | solution.py:58
  (1 shorter events, 0.0 us)
Async XLA Ops:
  6.5 76.5 %copy-start = (bf16[1,1024,1024]{2,1,0:T(8,128)(2,1)S(1)}, bf16[1,1024,1024]{2,1,0:T(8,128)(2,1)}, u32[]{:S(2)}) copy-start(bf16[1,1024,1024]{2,1,0:T(8,128)(2,1)} %param.14) | copy-start | bytes 6291460
  6.5 24.7 %all-gather.6.cloned.1.call-start = ((), (), s32[]{:S(2)}) async-start(), calls=%async_computation.7 | async-start | bytes 1966080 | tf_op jit(solution)/shard_map/all_gather | solution.py:16
  7.3 75.8 %all-gather.4.cloned.1.call-start = ((), (), s32[]{:S(2)}) async-start(), calls=%async_computation.5 | async-start | bytes 2457600 | tf_op jit(solution)/shard_map/all_gather | solution.py:44
  36.4 3.6 %copy-start.2 = (f32[1024]{0:T(1024)S(1)}, f32[1024]{0:T(1024)}, u32[]{:S(2)}) copy-start(f32[1024]{0:T(1024)} %param.10) | copy-start | bytes 12292
  42.2 1.2 copy-start.1
  62.7 58.7 %reduce-scatter.5.cloned.1.call-start = ((), (), s32[]{:S(2)}) async-start(), calls=%async_computation.6 | async-start | bytes 2457600 | tf_op jit(solution)/shard_map/reduce_scatter | solution.py:50
  90.9 61.0 %copy-start.3 = (f32[768]{0:T(1024)S(1)}, f32[768]{0:T(1024)}, u32[]{:S(2)}) copy-start(f32[768]{0:T(1024)} %param.17) | copy-start | bytes 9220
  90.9 60.9 %reduce-scatter.3.cloned.1.call-start = ((), (), s32[]{:S(2)}) async-start(), calls=%async_computation.4 | async-start | bytes 1966080 | tf_op jit(solution)/shard_map/reduce_scatter | solution.py:63
  121.5 30.4 %all-to-all-start.1 = ((bf16[4,240,256]{2,1,0:T(8,128)(2,1)}), bf16[4,240,256]{2,1,0:T(8,128)(2,1)S(1)}, u32[]{:S(2)}, u32[]{:S(2)}) async-start(bf16[4,240,256]{2,1,0:T(8,128)(2,1)} %bitcast.33), calls=%async_computation.3 | async-start | bytes 983040 | tf_op jit(solution)/shard_map/all_to_all | solution.py:51
Sparse Core Ops, SparseCore 0:
  8.9 22.3 all-gather.5
  62.8 20.1 all-gather.3
  91.0 30.3 reduce-scatter.4
  123.8 27.9 reduce-scatter.2
